TPU v7x, 32 devices: a whole 2x2x4 slice. The times are simulated.
32 devices in a mesh: dom: 32 (over z, y, x, core).
Axes of the slice: x: 2, y: 2, z: 4, core: 2. Of those that a mesh axis runs over, the one named last changes fastest.
Arguments:
- particles: bfloat16 [1024, 2, 7488], P('dom'), may hold values from -6 to 6
- references: bfloat16 [32, 2, 7488], P('dom'), may hold values from -6 to 6
- assignment: int32 [1024, 1], P('dom'), may hold values from 0 to 31
- orientation: int32 [1024], P('dom'), may hold values from 0 to 35
- tilt_range: int32 [2, 1024], P(None, 'dom'), may hold values from 0 to 20
Outputs:
- scores: float32 [1024, 32], P('dom')
- class_means: float32 [32, 2, 7488], P('dom')
- class_load: float32 [32], replicated
Inputs may be any that keep to these rules, and one draw needn't show every extreme that they name: `assignment`: every class has at least one particle.
All inputs are finite; a program needn't handle non-finite values.
Results may differ from a plain program's by a relative error of at most 0.0035.
Values may be sent and summed in bfloat16 or wider, within the bound.
A program may use at most 128 MiB of HBM per device.

v0:
```python
import math

import jax
import jax.numpy as jnp
from jax import lax
from jax.sharding import PartitionSpec as P

GRID = 24
ORIENTS = 36
COEF = 7488


EPS = 1e-06
GAIN = 6.0
TAU = 0.5
member_rows = 256


def tables():
    index = jnp.arange(COEF, dtype=jnp.int32)
    plane = index // (GRID * GRID)
    rest = index % (GRID * GRID)
    col_x = rest // GRID
    col_z = rest % GRID
    freq_x = ((col_x + GRID // 2) % GRID - GRID // 2).astype(jnp.float32)
    freq_y = plane.astype(jnp.float32)
    freq_z = ((col_z + GRID // 2) % GRID - GRID // 2).astype(jnp.float32)
    return (freq_x, freq_y, freq_z)


def wedge_weights(orient, low_bin, high_bin):
    freq_x, freq_y, freq_z = tables()
    angle = orient.astype(jnp.float32) * (2.0 * math.pi / ORIENTS)
    along = -freq_x[None, :] * jnp.sin(angle)[:, None] + freq_y[None, :] * jnp.cos(angle)[:, None]
    radius = along * along + freq_z[None, :] * freq_z[None, :] + 1.0
    cos_two = (along * along - freq_z[None, :] * freq_z[None, :]) / radius
    sin_two = -2.0 * along * freq_z[None, :] / radius
    low = -(40.0 + 1.5 * low_bin.astype(jnp.float32)) * (math.pi / 180.0)
    high = (40.0 + 1.5 * high_bin.astype(jnp.float32)) * (math.pi / 180.0)
    centre = (low + high)[:, None]
    width = (high - low)[:, None]
    return jax.nn.sigmoid(
        GAIN * (cos_two * jnp.cos(centre) + sin_two * jnp.sin(centre) - jnp.cos(width))
    )


def body(particles, references, assignment, orientation, tilt_range):
    part_rows = particles.shape[0]
    coef = particles.shape[2]
    owned = references.shape[0]
    devices = lax.axis_size("dom")
    classes = owned * devices
    total = part_rows * devices
    cls = assignment[:, 0]
    wedge = wedge_weights(orientation, tilt_range[0], tilt_range[1])
    pf = particles.astype(jnp.float32)
    weighted = (wedge[:, None, :] * pf).astype(jnp.bfloat16)
    flat = weighted.reshape(part_rows, 2 * coef)
    wedge_low = wedge.astype(jnp.bfloat16)
    power = jnp.sum(wedge * (pf[:, 0] * pf[:, 0] + pf[:, 1] * pf[:, 1]), axis=1)
    piece = lax.all_gather(references, "dom", axis=0, tiled=True)
    count = piece.shape[0]
    p32 = piece.astype(jnp.float32)
    ref_power = (p32[:, 0] * p32[:, 0] + p32[:, 1] * p32[:, 1]).astype(jnp.bfloat16)
    intersection = lax.dot_general(
        flat,
        piece.reshape(count, 2 * coef),
        (((1,), (1,)), ((), ())),
        preferred_element_type=jnp.float32,
    )
    energy = lax.dot_general(
        wedge_low, ref_power, (((1,), (1,)), ((), ())), preferred_element_type=jnp.float32
    )
    scores = intersection / (
        math.sqrt(coef) * jnp.sqrt((energy / coef + EPS) * (power[:, None] / coef + EPS))
    )
    ids = lax.iota(jnp.int32, owned * lax.axis_size("dom"))
    onehot = (ids[:, None] == cls[None, :]).astype(jnp.bfloat16)
    numer = lax.psum_scatter(
        jnp.dot(onehot, flat, preferred_element_type=jnp.float32),
        "dom",
        scatter_dimension=0,
        tiled=True,
    )
    labels = jnp.stack([cls, orientation, tilt_range[0], tilt_range[1]])
    every = lax.all_gather(labels, "dom", axis=1, tiled=True)
    class_ids = jnp.arange(classes, dtype=jnp.int32)
    counts = jnp.sum((class_ids[:, None] == every[0][None, :]).astype(jnp.float32), axis=1)
    own_class = lax.axis_index("dom") * owned + 0
    chosen = every[0] == own_class
    members = jnp.nonzero(chosen, size=total + member_rows, fill_value=0)[0].astype(jnp.int32)
    members_count = jnp.sum(chosen.astype(jnp.int32))
    block_count = (members_count + member_rows - 1) // member_rows

    def member_block(block, acc):
        square_sum, wedge_sum = acc
        first = (block * member_rows).astype(jnp.int32)
        picked = lax.dynamic_slice_in_dim(members, first, member_rows, 0)
        valid = (first + lax.iota(jnp.int32, member_rows) < members_count).astype(jnp.float32)
        member_wedge = wedge_weights(every[1][picked], every[2][picked], every[3][picked])
        squares = (member_wedge * member_wedge).astype(jnp.bfloat16).astype(jnp.float32)
        square_sum = square_sum + jnp.sum(valid[:, None] * squares, axis=0)
        wedge_sum = wedge_sum + jnp.sum(valid * jnp.sum(member_wedge, axis=1))
        return (square_sum, wedge_sum)

    square_sum, wedge_sum = lax.fori_loop(
        0, block_count, member_block, (jnp.zeros((coef,), jnp.float32), jnp.zeros((), jnp.float32))
    )
    denom_rows = [square_sum]
    total_rows = [wedge_sum]
    denom = jnp.stack(denom_rows)
    own_totals = jnp.stack(total_rows)
    bottom = denom + TAU * (own_totals[:, None] / coef + 1.0)
    class_means = numer.reshape(owned, 2, coef) / bottom[:, None, :]
    class_load = counts * classes / total
    return (scores, class_means, class_load)


def solution(mesh):
    in_specs = (
        P("dom", None, None),
        P("dom", None, None),
        P("dom", None),
        P("dom"),
        P(None, "dom"),
    )
    out_specs = (P("dom", None), P("dom", None, None), P())
    return jax.shard_map(body, mesh=mesh, in_specs=in_specs, out_specs=out_specs, check_vma=False)
```

profile of v0, /device:TPU:0, one launch (start us, length us, event | category | flops | bytes accessed | tf_op | source)
XLA Modules:
  0.0 159.8 jit_solution(15406478561462494399)
XLA Ops:
  7.2 0.0 all-reduce.3.cloned.1.call-start
  7.2 0.1 fusion.46
  7.3 0.1 fusion.61
  7.4 1.3 copy_convert_fusion
  8.8 0.0 copy-start
  8.8 0.1 cosine_bitcast_fusion.1
  8.9 1.1 fusion.34
  10.0 0.0 copy-done
  10.0 0.2 multiply_convert_fusion.1
  10.1 0.0 copy-start.3
  10.1 0.7 copy.29
  10.9 0.7 reshape.483
  11.6 0.0 copy-start.1
  11.7 1.7 %fusion.62 = f32[32,14976]{1,0:T(8,128)} fusion(bf16[32,14976]{1,0:T(8,128)(2,1)S(1)} %reshape.483, s32[32]{0:T(128)S(1)} %bitcast.59), kind=kOutput, calls=%fused_computation.115 | convolution fusion | flops 30671872 | bytes 2875520 | tf_op jit(solution)/shard_map/dot_general | solution.py:80
  13.3 0.0 all-reduce.3.cloned.1.call-update
  13.3 47.1 %all_gather.6 = bf16[32,2,7488]{2,1,0:T(2,128)(2,1)S(1)} all-gather(bf16[1,2,7488]{2,1,0:T(2,128)(2,1)S(1)} %copy-done.1), channel_id=1, replica_groups=mesh['dom'=32] {'dom'}, dimensions={0}, use_global_device_ids=true | all-gather | bytes 988416 | tf_op jit(solution)/shard_map/all_gather | solution.py:61
  60.4 0.4 convolution_bitcast_fusion
  60.8 0.1 copy_convert_fusion.1
  61.0 36.9 %all-gather = s32[32,32,4]{1,2,0:T(4,128)S(1)} all-gather(s32[1,32,4]{1,2,0:T(4,128)S(1)} %add_bitcast_fusion), channel_id=1, replica_groups=mesh['dom'=32] {'dom'}, dimensions={0}, use_global_device_ids=true | all-gather | bytes 16896 | tf_op jit(solution)/shard_map/all_gather | solution.py:86
  97.9 0.1 reshape.532
  98.0 0.6 convert_reduce_fusion.1
  99.3 0.1 convert_reduce_fusion
  99.4 0.3 reduce-window.16
  99.7 0.1 slice.71
  99.8 0.1 slice_reduce_fusion.1
  99.9 0.1 broadcast_add_fusion.1
  100.0 7.6 %scatter_custom_fusion = s32[1280]{0:T(1024)S(1)} fusion(s32[1024]{0:T(1024)S(1)} %bitcast.58, s32[1024]{0:T(1024)S(1)} %broadcast.1000, s32[]{:T(128)} %constant.257.clone.1), kind=kCustom, calls=%fused_computation.126 | custom fusion | flops 1024 | bytes 5124 | tf_op jit(solution)/shard_map/scatter-add | solution.py:91
  107.7 0.3 reduce-window.24
  107.9 0.1 slice.87
  108.0 0.1 slice_reduce_fusion
  108.2 0.7 fusion.64
  108.9 13.8 %while.15 = (s32[]{:T(128)}, f32[7488]{0:T(1024)S(1)}, f32[]{:T(128)}, s32[]{:T(128)}, s32[]{:T(128)}, /*index=5*/s32[4,1024]{1,0:T(4,128)S(1)}, s32[1280]{0:T(1...) while((s32[]{:T(128)}, f32[7488]{0:T(1024)S(1)}, f32[]{:T(128)}, s32[]{:T(128)}, s32[]{:T(128)}, ...), condition=%wide.region_12.13_spmd, body=%wide.region_8.12_spmd.sunk | while | flops 46529604 | bytes 420039 | solution.py:106
  109.1 0.1 compare_select_fusion.3
  109.2 1.4 gather_fusion
  110.6 1.4 gather_fusion.1
  112.0 1.4 gather_fusion.2
  113.3 0.1 fusion.83
  113.4 0.1 fusion.84
  113.5 0.1 fusion.85
  113.6 0.7 fusion.87
  114.3 6.5 %fusion.88 = (f32[256]{0:T(256)S(1)}, f32[7488]{0:T(1024)S(1)}) fusion(f32[256]{0:T(256)S(1)} %get-tuple-element.240, f32[256]{0:T(256)S(1)} %sin.43, f32[7488]{0:T(1024)S(1)} %get-tuple-element.242, f32[256]{0:T(256)S(1)} %get-tuple-element.243, f32[7488]{0:T(1024)S(1)} %fusion.85, f32[256]{0:T(256)S(1)} %get-tuple-element.244, f32[7488]{0:T(1024)S(1)} %fusion.86, ...), kind=kLoop, calls=%fused_computation.7.clone.1 | loop fusion | flops 45998528 | bytes 156928 | tf_op jit(solution)/shard_map/while/body/reduce_sum | solution.py:103
  120.8 1.3 select_reduce_fusion.2
  122.7 0.5 broadcast_multiply_fusion.2
  123.2 1.6 fusion.30
  124.8 26.2 %all-reduce.3.cloned.1.call-done = f32[32,14976]{1,0:T(8,128)} async-done(((f32[32,14976]{1,0:T(8,128)}), f32[32,14976]{1,0:T(8,128)}) %all-reduce.3.cloned.1.call-update) | async-done | bytes 1916944
  151.0 1.2 dynamic-slice_reduce_fusion
  152.1 0.1 reshape.484
  152.3 0.7 broadcast_divide_fusion
  (24 shorter events, 0.3 us)
Async XLA Ops:
  7.2 1.6 copy-start.2
  7.2 1.7 %copy-start.4 = (s32[32]{0:T(128)S(1)}, s32[32]{0:T(128)}, u32[]{:S(2)}) copy-start(s32[32]{0:T(128)} %param.10) | copy-start | bytes 388
  7.2 143.8 %all-reduce.3.cloned.1.call-start = ((), (), s32[]{:S(2)}) async-start(), calls=%async_computation | async-start | bytes 3833856
  8.8 1.2 copy-start
  10.1 1.5 copy-start.3
  11.6 1.7 %copy-start.1 = (bf16[1,2,7488]{2,1,0:T(2,128)(2,1)S(1)}, bf16[1,2,7488]{2,1,0:T(2,128)(2,1)}, u32[]{:S(2)}) copy-start(bf16[1,2,7488]{2,1,0:T(2,128)(2,1)} %param.8) | copy-start | bytes 89860
Sparse Core Ops, SparseCore 0:
  13.5 137.4 all-reduce.2
where the time goes:
time: 160 us
  blocking collectives  84 us (52%)
  waiting for transfers between devices  26.2 us (16%)
  other arithmetic  22.7 us (14%)
  between operations  14.9 us (9%)
  local copies, waits for them, and re-layouts  7.43 us (5%)
  matrix products  3.61 us (2%)
    all_gather x1, blocking collectives, body(): piece = lax.all_gather(references, 'dom', axis=0, tiled=True)  47.1 us
    all_gather x1, blocking collectives, body(): every = lax.all_gather(labels, 'dom', axis=1, tiled=True)  36.9 us
    unnamed x2, waiting for transfers between devices  26.2 us
    reduce_sum x2, other arithmetic, member_block(): wedge_sum = wedge_sum + jnp.sum(valid * jnp.sum(member_wedge, axis=1))  7.77 us
    scatter-add x1, other arithmetic, body(): jnp.nonzero(chosen, size=total + member_rows, fill_value=0)[0]  7.63 us
  transfers between devices with their start and end apart: 1, of which 1 were waited for; matrix products, arithmetic and copies ran while one was open for 16% of the time, Pallas kernels for 0%

commit v1 on v0

v1 whole, which is shorter than its diff:
```python
import functools
import math

import jax
import jax.numpy as jnp
from jax import lax
from jax.experimental import pallas as pl
from jax.experimental.pallas import tpu as pltpu
from jax.sharding import PartitionSpec as P

GRID = 24
ORIENTS = 36
EPS = 1e-06
GAIN = 6.0
TAU = 0.5
LANES = 128
MESH = pl.DeviceIdType.MESH


def tables(coef):
    index = jnp.arange(coef, dtype=jnp.int32)
    plane = index // (GRID * GRID)
    rest = index % (GRID * GRID)
    col_x = rest // GRID
    col_z = rest % GRID
    freq_x = ((col_x + GRID // 2) % GRID - GRID // 2).astype(jnp.float32)
    freq_y = plane.astype(jnp.float32)
    freq_z = ((col_z + GRID // 2) % GRID - GRID // 2).astype(jnp.float32)
    return (freq_x, freq_y, freq_z)


def wedge_weights(orient, low_bin, high_bin, coef):
    freq_x, freq_y, freq_z = tables(coef)
    angle = orient.astype(jnp.float32) * (2.0 * math.pi / ORIENTS)
    along = -freq_x[None, :] * jnp.sin(angle)[:, None] + freq_y[None, :] * jnp.cos(angle)[:, None]
    radius = along * along + freq_z[None, :] * freq_z[None, :] + 1.0
    cos_two = (along * along - freq_z[None, :] * freq_z[None, :]) / radius
    sin_two = -2.0 * along * freq_z[None, :] / radius
    low = -(40.0 + 1.5 * low_bin.astype(jnp.float32)) * (math.pi / 180.0)
    high = (40.0 + 1.5 * high_bin.astype(jnp.float32)) * (math.pi / 180.0)
    centre = (low + high)[:, None]
    width = (high - low)[:, None]
    return jax.nn.sigmoid(
        GAIN * (cos_two * jnp.cos(centre) + sin_two * jnp.sin(centre) - jnp.cos(width))
    )


def factor(devices):
    chips = devices // 2
    inner = 1
    while inner * inner < chips:
        inner *= 2
    return chips // inner, inner


def kernel(
    outer, inner, half, coef,
    data_ref, onehot_ref, small_ref, ref_ref,
    all_ref, means_ref, sums_ref,
    mine, send_core, recv_core, send_in, recv_in, send_out, recv_out, small_send, small_recv,
    ag_send_out, ag_send_in, ag_send_core, ag_recv,
    core_sems, in_send_sems, in_recv_sems, out_send_sems, out_recv_sems,
    small_send_sems, small_recv_sems, local_sem,
):
    me = lax.axis_index("dom")
    core = lax.rem(me, 2)
    chip = me // 2
    b = lax.rem(chip, inner)
    a = chip // inner
    sibling = me + 1 - 2 * core

    def device(a_at, b_at, c_at):
        return (a_at * inner + b_at) * 2 + c_at

    def in_peer(j):
        return device(a, lax.rem(b + j, inner), core)

    def out_peer(i):
        return device(lax.rem(a + i, outer), b, core)

    barrier = pltpu.get_barrier_semaphore()
    pl.semaphore_signal(barrier, inc=1, device_id=(sibling,), device_id_type=MESH)
    for j in range(1, inner):
        pl.semaphore_signal(barrier, inc=1, device_id=(in_peer(j),), device_id_type=MESH)
    for i in range(1, outer):
        pl.semaphore_signal(barrier, inc=1, device_id=(out_peer(i),), device_id_type=MESH)

    part = 2 * outer * inner // 2
    step = half
    for t in range(6):
        cols = pl.ds(t * step, step)
        sums = jnp.dot(onehot_ref[...], data_ref[:, cols], preferred_element_type=jnp.float32)
        mine[:, cols] = sums[:part]
        send_core[:, cols] = sums[part:].astype(jnp.bfloat16)
    small_send[0] = small_ref[...]

    pl.semaphore_wait(barrier, 1 + (inner - 1) + (outer - 1))

    def push(src, dst, send_sem, recv_sem, target):
        copy = pltpu.make_async_remote_copy(
            src_ref=src, dst_ref=dst, send_sem=send_sem, recv_sem=recv_sem,
            device_id=(target,), device_id_type=MESH,
        )
        copy.start()
        return copy

    pending = []
    core_copy = push(send_core, recv_core, core_sems.at[0], core_sems.at[1], sibling)
    small_core = push(small_send.at[0], small_recv.at[0], small_send_sems.at[0], small_recv_sems.at[0], sibling)

    local = pltpu.make_async_copy(ref_ref.at[0], all_ref.at[me], local_sem)
    local.start()
    for i in range(1, outer):
        pending.append(push(ref_ref.at[0], all_ref.at[me], ag_send_out.at[i - 1], ag_recv.at[me], out_peer(i)))
    for j in range(1, inner):
        pending.append(push(ref_ref.at[0], all_ref.at[me], ag_send_in.at[0, j - 1], ag_recv.at[me], in_peer(j)))
    pending.append(push(ref_ref.at[0], all_ref.at[me], ag_send_core.at[0], ag_recv.at[me], sibling))

    def arrived(place):
        pltpu.make_async_remote_copy(
            src_ref=all_ref.at[place], dst_ref=all_ref.at[place],
            send_sem=local_sem, recv_sem=ag_recv.at[place],
            device_id=(sibling,), device_id_type=MESH,
        ).wait_recv()

    core_copy.wait_recv()
    small_core.wait_recv()
    small_send[1] = small_send[0] + small_recv[0]
    for j in range(1, inner):
        rows = slice(j * outer, (j + 1) * outer)
        send_in[j - 1] = (mine[rows] + recv_core[rows].astype(jnp.float32)).astype(jnp.bfloat16)
    in_copies = []
    for j in range(1, inner):
        in_copies.append(push(send_in.at[j - 1], recv_in.at[j - 1], in_send_sems.at[j - 1], in_recv_sems.at[j - 1], in_peer(j)))
        in_copies.append(push(small_send.at[1], small_recv.at[j], small_send_sems.at[j], small_recv_sems.at[j], in_peer(j)))
    total = mine[:outer] + recv_core[:outer].astype(jnp.float32)
    mine[:outer] = total

    for i in range(1, outer):
        place = device(lax.rem(a + outer - i, outer), b, core)
        arrived(place)
        for j in range(1, inner):
            pending.append(push(all_ref.at[place], all_ref.at[place], ag_send_in.at[i, j - 1], ag_recv.at[place], in_peer(j)))
        pending.append(push(all_ref.at[place], all_ref.at[place], ag_send_core.at[i], ag_recv.at[place], sibling))

    for copy in in_copies:
        copy.wait_recv()
    row = small_send[1]
    for j in range(1, inner):
        row = row + small_recv[j]
    small_send[2] = row
    for i in range(1, outer):
        pieces = []
        for h in range(2):
            cols = slice(h * 3 * half, (h + 1) * 3 * half)
            piece = mine[i:i + 1, cols]
            for j in range(1, inner):
                piece = piece + recv_in[j - 1, :, cols].astype(jnp.float32)[i:i + 1]
            pieces.append(piece)
        send_out[i - 1] = jnp.concatenate(pieces, axis=0).astype(jnp.bfloat16)
    out_copies = []
    for i in range(1, outer):
        out_copies.append(push(send_out.at[i - 1], recv_out.at[i - 1], out_send_sems.at[i - 1], out_recv_sems.at[i - 1], out_peer(i)))
        out_copies.append(push(small_send.at[2], small_recv.at[inner + i - 1], small_send_sems.at[inner + i - 1], small_recv_sems.at[inner + i - 1], out_peer(i)))
    pieces = []
    for h in range(2):
        cols = slice(h * 3 * half, (h + 1) * 3 * half)
        piece = mine[0:1, cols]
        for j in range(1, inner):
            piece = piece + recv_in[j - 1, :, cols].astype(jnp.float32)[0:1]
        pieces.append(piece)
    own = jnp.concatenate(pieces, axis=0)

    slot = outer
    for i in range(outer):
        for j in range(1, inner):
            place = device(lax.rem(a + outer - i, outer), lax.rem(b + inner - j, inner), core)
            arrived(place)
            pending.append(push(all_ref.at[place], all_ref.at[place], ag_send_core.at[slot], ag_recv.at[place], sibling))
            slot += 1

    for copy in out_copies:
        copy.wait_recv()
    for i in range(1, outer):
        own = own + recv_out[i - 1].astype(jnp.float32)
        row = row + small_recv[inner + i - 1]
    sums_ref[...] = row
    classes = 2 * outer * inner
    lane = lax.broadcasted_iota(jnp.int32, row.shape, 1)
    wedge_total = jnp.sum(jnp.where(lane == classes + me, row, 0.0), axis=1, keepdims=True)
    scale = 1.0 / (own[:, 2 * half:] + TAU * (wedge_total / coef + 1.0))
    for part_at in range(2):
        mean = own[:, part_at * half:(part_at + 1) * half] * scale
        means_ref[0, part_at:part_at + 1, 0:half] = mean[0:1]
        means_ref[0, part_at:part_at + 1, half:coef] = mean[1:2, :coef - half]

    for i in range(outer):
        for j in range(inner):
            arrived(device(lax.rem(a + i, outer), lax.rem(b + j, inner), 1 - core))
    local.wait()
    for copy in pending + [core_copy, small_core] + in_copies + out_copies:
        copy.wait_send()


def body(particles, references, assignment, orientation, tilt_range):
    part_rows = particles.shape[0]
    coef = particles.shape[2]
    devices = lax.axis_size("dom")
    classes = references.shape[0] * devices
    assert references.shape[0] == 1
    outer, inner = factor(devices)
    total = part_rows * devices
    half = -(-coef // (2 * LANES)) * LANES
    me = lax.axis_index("dom")
    cls = assignment[:, 0]
    wedge = wedge_weights(orientation, tilt_range[0], tilt_range[1], coef)
    pf = particles.astype(jnp.float32)
    weighted = (wedge[:, None, :] * pf).astype(jnp.bfloat16)
    wedge_low = wedge.astype(jnp.bfloat16)
    wedge_sq = (wedge * wedge).astype(jnp.bfloat16)
    power = jnp.sum(wedge * (pf[:, 0] * pf[:, 0] + pf[:, 1] * pf[:, 1]), axis=1)
    stacked = [jnp.pad(x, ((0, 0), (0, 2 * half - coef))) for x in (weighted[:, 0], weighted[:, 1], wedge_sq)]
    data = jnp.concatenate([x[:, :half] for x in stacked] + [x[:, half:] for x in stacked], axis=1)

    core, chip = me % 2, me // 2
    b, a = chip % inner, chip // inner
    row = jnp.arange(classes, dtype=jnp.int32)
    flip, rest = row // (classes // 2), row % (classes // 2)
    ids = (((a + rest % outer) % outer) * inner + (b + rest // outer) % inner) * 2 + (core + flip) % 2
    onehot = (ids[:, None] == cls[None, :]).astype(jnp.bfloat16)
    hits = (row[:, None] == cls[None, :]).astype(jnp.float32)
    width = -(-2 * classes // LANES) * LANES
    small = jnp.concatenate([
        jnp.sum(hits, axis=1), jnp.sum(hits * jnp.sum(wedge, axis=1)[None, :], axis=1),
        jnp.zeros((width - 2 * classes,), jnp.float32),
    ])[None, :]

    vmem = pl.BlockSpec(memory_space=pltpu.VMEM)
    dma = pltpu.SemaphoreType.DMA
    piece, means, sums = pl.pallas_call(
        functools.partial(kernel, outer, inner, half, coef),
        out_shape=(
            jax.ShapeDtypeStruct((classes, 2, coef), jnp.bfloat16),
            jax.ShapeDtypeStruct((1, 2, coef), jnp.float32),
            jax.ShapeDtypeStruct((1, width), jnp.float32),
        ),
        in_specs=[vmem] * 4,
        out_specs=(vmem, vmem, vmem),
        scratch_shapes=[
            pltpu.VMEM((classes // 2, 6 * half), jnp.float32),
            pltpu.VMEM((classes // 2, 6 * half), jnp.bfloat16),
            pltpu.VMEM((classes // 2, 6 * half), jnp.bfloat16),
            pltpu.VMEM((inner - 1, outer, 6 * half), jnp.bfloat16),
            pltpu.VMEM((inner - 1, outer, 6 * half), jnp.bfloat16),
            pltpu.VMEM((outer - 1, 2, 3 * half), jnp.bfloat16),
            pltpu.VMEM((outer - 1, 2, 3 * half), jnp.bfloat16),
            pltpu.VMEM((3, 1, width), jnp.float32),
            pltpu.VMEM((inner + outer - 1, 1, width), jnp.float32),
            dma((outer,)), dma((outer, inner)), dma((outer * inner,)), dma((classes,)),
            dma((2,)), dma((inner,)), dma((inner,)), dma((outer,)), dma((outer,)),
            dma((inner + outer,)), dma((inner + outer,)), dma,
        ],
        compiler_params=pltpu.CompilerParams(
            collective_id=0, has_side_effects=True, vmem_limit_bytes=60 * 1024 * 1024
        ),
    )(data, onehot, small, references)

    p32 = piece.astype(jnp.float32)
    ref_power = (p32[:, 0] * p32[:, 0] + p32[:, 1] * p32[:, 1]).astype(jnp.bfloat16)
    intersection = lax.dot_general(
        weighted.reshape(part_rows, 2 * coef), piece.reshape(classes, 2 * coef),
        (((1,), (1,)), ((), ())), preferred_element_type=jnp.float32,
    )
    energy = lax.dot_general(
        wedge_low, ref_power, (((1,), (1,)), ((), ())), preferred_element_type=jnp.float32
    )
    scores = intersection / (
        math.sqrt(coef) * jnp.sqrt((energy / coef + EPS) * (power[:, None] / coef + EPS))
    )
    class_load = sums[0, :classes] * classes / total
    return (scores, means, class_load)


def solution(mesh):
    in_specs = (
        P("dom", None, None),
        P("dom", None, None),
        P("dom", None),
        P("dom"),
        P(None, "dom"),
    )
    out_specs = (P("dom", None), P("dom", None, None), P())
    return jax.shard_map(body, mesh=mesh, in_specs=in_specs, out_specs=out_specs, check_vma=False)
```

time: 160 us -> 40.7 us (0.25)
  blocking collectives: 84 us -> 0 us
  Pallas kernels: 0 us -> 26.7 us
  waiting for transfers between devices: 26.2 us -> 0 us
  between operations: 14.9 us -> 0.86 us
  other arithmetic: 22.7 us -> 9.56 us
  local copies, waits for them, and re-layouts: 7.43 us -> 1.4 us
  matrix products: 3.61 us -> 1.89 us
    all_gather x2 -> x0, blocking collectives: 84 us -> none  [the longest x1 47.1 us: body(): piece = lax.all_gather(references, 'dom', axis=0, tiled=True)]
    pallas_call x0 -> x1, Pallas kernels: none -> 26.7 us  [body(): pl.pallas_call(functools.partial(kernel, outer, inner, half, coef), out_s...]
    unnamed x2 -> x0, waiting for transfers between devices: 26.2 us -> none
    reduce_sum x4 -> x1, other arithmetic: 8.53 us -> 0.11 us  [body(): jnp.sum(hits, axis=1)]
    scatter-add x1 -> x0, other arithmetic: 7.63 us -> none  [body(): jnp.nonzero(chosen, size=total + member_rows, fill_value=0)[0]]
    gather x3 -> x0, local copies, waits for them, and re-layouts: 4.09 us -> none  [the longest x1 1.37 us: member_block(): every[3][picked]]
    convert_element_type x1, other arithmetic: 0.13 us -> 1.86 us  [body(): p32 = piece.astype(jnp.float32)]
    dot_general x2 -> x1, matrix products: 2.05 us -> 0.39 us  [body(): lax.dot_general(weighted.reshape(part_rows, 2 * coef), piece.reshape(clas...]
  transfers between devices with their start and end apart: 1 -> 0, of which waited for: 1 -> 0; matrix products, arithmetic and copies ran while one was open for 16% -> 0% of each run, Pallas kernels for 0% -> 0%
where the time goes in v1:
time: 40.7 us; the launch traced here: 40.4 us
  Pallas kernels  26.7 us (66%)
  other arithmetic  9.56 us (23%)
  matrix products  1.89 us (5%)
  local copies, waits for them, and re-layouts  1.4 us (3%)
  between operations  0.86 us (2%)
    pallas_call x1, Pallas kernels, body(): pl.pallas_call(functools.partial(kernel, outer, inner, half, coef), out_s...  26.7 us
    convert_element_type x1, other arithmetic, body(): p32 = piece.astype(jnp.float32)  1.86 us
    convert_element_type x1, other arithmetic, body(): (p32[:, 0] * p32[:, 0] + p32[:, 1] * p32[:, 1]).astype(jnp.bfloat16)  1.55 us
    dot_general x1, matrix products, body(): lax.dot_general(wedge_low, ref_power, (((1,), (1,)), ((), ())), preferred...  1.5 us
    convert_element_type x1, other arithmetic, body(): pf = particles.astype(jnp.float32)  1.32 us
    unnamed x18, local copies, waits for them, and re-layouts  1.31 us
    reduce_sum x1, other arithmetic, body(): power = jnp.sum(wedge * (pf[:, 0] * pf[:, 0] + pf[:, 1] * pf[:, 1]), axis=1)  1.08 us

profile of v1, /device:TPU:0, one launch (start us, length us, event | category | flops | bytes accessed | tf_op | source)
XLA Modules:
  0.0 40.4 jit_solution(8124385957313153581)
XLA Ops:
  0.6 0.8 %cosine_bitcast_fusion.1 = (f32[32]{0:T(128)S(1)}, f32[32]{0:T(128)S(1)}, f32[32]{0:T(128)S(1)}) fusion(s32[2,32]{1,0:T(2,128)} %param.9), kind=kLoop, calls=%fused_computation.101 | loop fusion | flops 352 | bytes 640 | tf_op jit(solution)/shard_map/cos | solution.py:44
  1.4 0.1 fusion.23
  1.5 0.7 %fusion.48 = (f32[32]{0:T(128)S(1)}, f32[32]{0:T(128)S(1)}) fusion(s32[32]{0:T(128)} %param.8), kind=kLoop, calls=%fused_computation.108 | loop fusion | flops 64 | bytes 384 | tf_op jit(solution)/shard_map/sin | solution.py:35
  2.3 0.1 fusion.38
  2.3 1.3 %copy_convert_fusion = f32[32,2,7488]{2,0,1:T(8,128)S(1)} fusion(bf16[32,2,7488]{2,1,0:T(2,128)(2,1)} %param.5), kind=kLoop, calls=%fused_computation.18 | loop fusion | flops 479232 | bytes 2875392 | tf_op jit(solution)/shard_map/convert_element_type | solution.py:217
  3.7 0.0 copy-start
  3.7 1.1 %fusion.8 = (f32[32]{0:T(128)S(1)}, f32[32]{0:T(128)S(1)}, bf16[32,7488]{1,0:T(8,128)(2,1)S(1)}, f32[32,7488]{1,0:T(8,128)S(1)}) fusion(f32[32,2,7488]{2,0,1:T(8,128)S(1)} %copy_convert_fusion, f32[32]{0:T(128)S(1)} %get-tuple-element.18, f32[32]{0:T(128)S(1)} %get-tuple-element.19, f32[7488]{0:T(1024)S(1)} %get-tuple-element.23, ...), kind=kLoop, calls=%fused_computation.12 | loop fusion | flops 6229952 | bytes 3475328 | tf_op jit(solution)/shard_map/reduce_sum | solution.py:221
  4.7 0.1 copy-done
  4.9 0.2 multiply_convert_fusion
  5.0 0.1 slice_bitcast_fusion
  5.1 0.0 copy-start.4
  5.3 0.0 copy-start.2
  5.4 0.5 %copy-done.4 = s32[32,1]{0,1:T(1,128)S(1)} copy-done((s32[32,1]{0,1:T(1,128)S(1)}, s32[32,1]{0,1:T(1,128)}, u32[]{:S(2)}) %copy-start.4) | copy-done | bytes 152
  5.8 0.7 %compare_convert_fusion.onehot_ref = bf16[32,32]{1,0:T(8,128)(2,1)} fusion(s32[32]{0:T(128)S(1)} %bitcast.27, s32[32]{0:T(128)S(1)} %fusion.40), kind=kLoop, calls=%fused_computation.71 | loop fusion | flops 2048 | bytes 2304 | tf_op jit(solution)/shard_map/convert_element_type | solution.py:230
  6.5 0.1 convert_reduce_fusion
  6.6 0.6 %maximum_bitcast_fusion.small_ref = f32[1,128]{1,0:T(1,128)} fusion(f32[64]{0:T(128)S(1)} %broadcast_in_dim.4, f32[32]{0:T(128)S(1)} %get-tuple-element.12, f32[32]{0:T(128)S(1)} %get-tuple-element.11), kind=kLoop, calls=%fused_computation.98 | loop fusion | flops 256 | bytes 1024 | tf_op jit(solution)/shard_map/broadcast_in_dim | solution.py:233
  7.2 0.0 copy-done.2
  7.2 26.7 %shard_map.76 = (bf16[32,2,7488]{2,1,0:T(2,128)(2,1)}, f32[1,2,7488]{2,1,0:T(2,128)}, f32[1,128]{1,0:T(1,128)}) custom-call(bf16[32,23040]{1,0:T(8,128)(2,1)} %copy-done.2, bf16[32,32]{1,0:T(8,128)(2,1)} %compare_convert_fusion.onehot_ref, f32[1,128]{1,0:T(1,128)} %maximum_bitcast_fusion.small_ref, bf16[1,2,7488]{2,1,0:T(2,128)(2,1)} %ref_ref.1), custom_call_target="tpu_custom_call" | custom-call | tf_op jit(solution)/shard_map/pallas_call | solution.py:240
  33.8 1.9 %convert_element_type.102 = f32[32,2,7488]{2,1,0:T(2,128)S(1)} convert(bf16[32,2,7488]{2,1,0:T(2,128)(2,1)} %get-tuple-element.6) | non-fusion elementwise | flops 479232 | bytes 2875392 | tf_op jit(solution)/shard_map/convert_element_type | solution.py:268
  35.7 0.0 copy-start.1
  35.7 1.5 %fusion.11 = bf16[32,1,7488]{2,1,0:T(2,128)(2,1)S(1)} fusion(f32[32,2,7488]{2,1,0:T(2,128)S(1)} %convert_element_type.102), kind=kLoop, calls=%fused_computation.21 | loop fusion | flops 958464 | bytes 2396160 | tf_op jit(solution)/shard_map/convert_element_type | solution.py:269
  37.3 0.0 copy-done.1
  37.3 0.4 convolution_bitcast_fusion
  37.7 0.0 copy-start.5
  37.7 0.0 copy-start.3
  37.7 1.5 %fusion.4 = f32[32,32]{1,0:T(8,128)} fusion(f32[32,32]{1,0:T(8,128)S(1)} %convolution_bitcast_fusion, bf16[32,1,7488]{2,1,0:T(2,128)(2,1)S(1)} %fusion.11, f32[32]{0:T(128)S(1)} %multiply_add_fusion, f32[32]{0:T(128)S(1)} %get-tuple-element.18, f32[32]{0:T(128)S(1)} %get-tuple-element.19, f32[7488]{0:T(1024)S(1)} %get-tuple-element.23, ...), kind=kOutput, calls=%fused_computation.6 | convolution fusion | flops 19893248 | bytes 608000 | tf_op jit(solution)/shard_map/dot_general | solution.py:274
  39.2 0.0 copy-done.5
  39.2 0.5 %multiply_bitcast_fusion = f32[32]{0:T(128)} fusion(f32[1,128]{1,0:T(1,128)S(1)} %copy-done.5), kind=kLoop, calls=%fused_computation.102 | loop fusion | flops 32 | bytes 256 | tf_op jit(solution)/shard_map/div | solution.py:280
  39.7 0.0 copy-done.3
  39.7 0.6 %copy.28 = f32[1,2,7488]{2,1,0:T(2,128)} copy(f32[1,2,7488]{2,1,0:T(2,128)S(1)} %copy-done.3) | data formatting | bytes 119808
  (10 shorter events, 0.2 us)
Async XLA Ops:
  3.7 1.2 %copy-start = (bf16[32,2,7488]{2,1,0:T(2,128)(2,1)S(1)}, bf16[32,2,7488]{2,1,0:T(2,128)(2,1)}, u32[]{:S(2)}) copy-start(bf16[32,2,7488]{2,1,0:T(2,128)(2,1)} %param.5) | copy-start | bytes 2875396
  5.1 0.7 %copy-start.4 = (s32[32,1]{0,1:T(1,128)S(1)}, s32[32,1]{0,1:T(1,128)}, u32[]{:S(2)}) copy-start(s32[32,1]{0,1:T(1,128)} %param.7) | copy-start | bytes 388
  5.3 1.9 %copy-start.2 = (bf16[32,23040]{1,0:T(8,128)(2,1)}, bf16[32,23040]{1,0:T(8,128)(2,1)S(1)}, u32[]{:S(2)}) copy-start(bf16[32,23040]{1,0:T(8,128)(2,1)S(1)} %fusion.17.data_ref) | copy-start | bytes 4423684
  35.7 1.6 %copy-start.1 = (bf16[32,2,7488]{2,1,0:T(2,128)(2,1)S(1)}, bf16[32,2,7488]{2,1,0:T(2,128)(2,1)}, u32[]{:S(2)}) copy-start(bf16[32,2,7488]{2,1,0:T(2,128)(2,1)} %get-tuple-element.6) | copy-start | bytes 2875396
  37.7 1.5 %copy-start.5 = (f32[1,128]{1,0:T(1,128)S(1)}, f32[1,128]{1,0:T(1,128)}, u32[]{:S(2)}) copy-start(f32[1,128]{1,0:T(1,128)} %get-tuple-element.8) | copy-start | bytes 1540
  37.7 2.0 %copy-start.3 = (f32[1,2,7488]{2,1,0:T(2,128)S(1)}, f32[1,2,7488]{2,1,0:T(2,128)}, u32[]{:S(2)}) copy-start(f32[1,2,7488]{2,1,0:T(2,128)} %get-tuple-element.28) | copy-start | bytes 179716

commit v2 on v1

v2 whole, which is shorter than its diff:
```python
import functools
import math

import jax
import jax.numpy as jnp
from jax import lax
from jax.experimental import pallas as pl
from jax.experimental.pallas import tpu as pltpu
from jax.sharding import PartitionSpec as P

GRID = 24
ORIENTS = 36
EPS = 1e-06
GAIN = 6.0
TAU = 0.5
LANES = 128
MESH = pl.DeviceIdType.MESH


def factor(devices):
    chips = devices // 2
    inner = 1
    while inner * inner < chips:
        inner *= 2
    return chips // inner, inner


CHUNKS = 3
SUB = 640


def column(row):
    rows = row.shape[1]
    line = lax.broadcasted_iota(jnp.int32, (rows, rows), 0)
    lane = lax.broadcasted_iota(jnp.int32, (rows, rows), 1)
    return jnp.sum(jnp.where(line == lane, row, 0.0), axis=1, keepdims=True)


def frequencies(first, width):
    index = (lax.broadcasted_iota(jnp.int32, (1, width), 1) + first).astype(jnp.float32)
    plane = jnp.floor((index + 0.5) * (1.0 / (GRID * GRID)))
    rest = index - plane * (GRID * GRID)
    col_x = jnp.floor((rest + 0.5) * (1.0 / GRID))
    col_z = rest - col_x * GRID
    freq_x = jnp.where(col_x >= GRID // 2, col_x - GRID, col_x)
    freq_z = jnp.where(col_z >= GRID // 2, col_z - GRID, col_z)
    return freq_x, plane, freq_z, index


def kernel(
    outer, inner, span, coef, total,
    part_ref, ref_ref, cls_ref, orient_ref, tilt_ref,
    scores_ref, means_ref, load_ref,
    data, low, all_ref, mine, send_core, recv_core, send_in, recv_in, send_out, recv_out,
    small_send, small_recv,
    ag_send_out, ag_send_in, ag_send_core, ag_recv,
    core_send_sems, core_recv_sems, in_send_sems, in_recv_sems, out_send_sems, out_recv_sems,
    small_send_sems, small_recv_sems, local_sem,
):
    me = lax.axis_index("dom")
    core = lax.rem(me, 2)
    chip = me // 2
    b = lax.rem(chip, inner)
    a = chip // inner
    sibling = me + 1 - 2 * core
    classes = 2 * outer * inner
    half = classes // 2
    rows = part_ref.shape[1]

    def device(a_at, b_at, c_at):
        return (a_at * inner + b_at) * 2 + c_at

    def in_peer(j):
        return device(a, lax.rem(b + j, inner), core)

    def out_peer(i):
        return device(lax.rem(a + i, outer), b, core)

    barrier = pltpu.get_barrier_semaphore()
    pl.semaphore_signal(barrier, inc=1, device_id=(sibling,), device_id_type=MESH)
    for j in range(1, inner):
        pl.semaphore_signal(barrier, inc=1, device_id=(in_peer(j),), device_id_type=MESH)
    for i in range(1, outer):
        pl.semaphore_signal(barrier, inc=1, device_id=(out_peer(i),), device_id_type=MESH)
    local = pltpu.make_async_copy(ref_ref.at[0], all_ref.at[me], local_sem)
    local.start()

    def push(src, dst, send_sem, recv_sem, target):
        copy = pltpu.make_async_remote_copy(
            src_ref=src, dst_ref=dst, send_sem=send_sem, recv_sem=recv_sem,
            device_id=(target,), device_id_type=MESH,
        )
        copy.start()
        return copy

    pending = []

    def arrived(place):
        pltpu.make_async_remote_copy(
            src_ref=all_ref.at[place], dst_ref=all_ref.at[place],
            send_sem=local_sem, recv_sem=ag_recv.at[place],
            device_id=(sibling,), device_id_type=MESH,
        ).wait_recv()

    angle = orient_ref[...].astype(jnp.float32) * (2.0 * math.pi / ORIENTS)
    bins = tilt_ref[...].astype(jnp.float32)
    low_end = -(40.0 + 1.5 * bins[0:1]) * (math.pi / 180.0)
    high_end = (40.0 + 1.5 * bins[1:2]) * (math.pi / 180.0)
    sin_a, cos_a = column(jnp.sin(angle)), column(jnp.cos(angle))
    cos_c = column(jnp.cos(low_end + high_end))
    sin_c = column(jnp.sin(low_end + high_end))
    cos_w = column(jnp.cos(high_end - low_end))
    cls_row = cls_ref[...].astype(jnp.float32)
    cls_col = column(cls_row)

    row = lax.broadcasted_iota(jnp.int32, (classes, 1), 0)
    log_outer = outer.bit_length() - 1
    log_half = half.bit_length() - 1
    row_i = row & (outer - 1)
    row_j = lax.shift_right_logical(row, log_outer) & (inner - 1)
    row_c = lax.shift_right_logical(row, log_half)
    ids = (((row_i + a) & (outer - 1)) * inner + ((row_j + b) & (inner - 1))) * 2 + ((row_c + core) & 1)
    onehot = jnp.where(ids.astype(jnp.float32) == cls_row, 1.0, 0.0).astype(jnp.bfloat16)

    wedge_sum = jnp.zeros((rows, 1), jnp.float32)
    power = jnp.zeros((rows, 1), jnp.float32)
    core_copies = []
    in_copies = [[] for _ in range(CHUNKS)]
    out_copies = [[] for _ in range(CHUNKS)]

    def inner_sends(t):
        core_copies[t].wait_recv()
        for j in range(1, inner):
            lines = slice(j * outer, (j + 1) * outer)
            send_in[t, j - 1] = (mine[t, lines] + recv_core[t, lines].astype(jnp.float32)).astype(jnp.bfloat16)
            in_copies[t].append(push(
                send_in.at[t, j - 1], recv_in.at[t, j - 1],
                in_send_sems.at[t, j - 1], in_recv_sems.at[t, j - 1], in_peer(j)))
        mine[t, :outer] = mine[t, :outer] + recv_core[t, :outer].astype(jnp.float32)

    def outer_sends(t):
        for copy in in_copies[t]:
            copy.wait_recv()
        piece = mine[t, :outer]
        for j in range(1, inner):
            piece = piece + recv_in[t, j - 1].astype(jnp.float32)
        wide = 3 * span // 2
        for i in range(1, outer):
            send_out[t, i - 1] = jnp.concatenate(
                [piece[i:i + 1, :wide], piece[i:i + 1, wide:]], axis=0).astype(jnp.bfloat16)
            out_copies[t].append(push(
                send_out.at[t, i - 1], recv_out.at[t, i - 1],
                out_send_sems.at[t, i - 1], out_recv_sems.at[t, i - 1], out_peer(i)))
        return jnp.concatenate([piece[0:1, :wide], piece[0:1, wide:]], axis=0)

    for t in range(CHUNKS):
        for s in range(span // SUB):
            first = t * span + s * SUB
            freq_x, freq_y, freq_z, index = frequencies(first, SUB)
            along = freq_y * cos_a - freq_x * sin_a
            along_sq = along * along
            z_sq = freq_z * freq_z
            scale = 1.0 / (along_sq + (z_sq + 1.0))
            value = ((along_sq - z_sq) * cos_c - (2.0 * along * freq_z) * sin_c) * scale - cos_w
            wedge = 1.0 / (1.0 + jnp.exp(value * (-GAIN)))
            real = part_ref[0, :, first:first + SUB].astype(jnp.float32)
            imag = part_ref[1, :, first:first + SUB].astype(jnp.float32)
            power = power + jnp.sum(wedge * (real * real + imag * imag), axis=1, keepdims=True)
            inside = wedge if first + SUB <= coef else jnp.where(index < coef, wedge, 0.0)
            wedge_sum = wedge_sum + jnp.sum(inside, axis=1, keepdims=True)
            at = s * SUB
            data[t, :, at:at + SUB] = (wedge * real).astype(jnp.bfloat16)
            data[t, :, span + at:span + at + SUB] = (wedge * imag).astype(jnp.bfloat16)
            data[t, :, 2 * span + at:2 * span + at + SUB] = (wedge * wedge).astype(jnp.bfloat16)
            low[:, first:first + SUB] = wedge.astype(jnp.bfloat16)
        for q in range(3):
            cols = slice(q * span, (q + 1) * span)
            sums = jnp.dot(onehot, data[t, :, cols], preferred_element_type=jnp.float32)
            send_core[t, :, cols] = sums[half:].astype(jnp.bfloat16)
            mine[t, :, cols] = sums[:half]
        if t == 0:
            pl.semaphore_wait(barrier, 1 + (inner - 1) + (outer - 1))
            for i in range(1, outer):
                pending.append(push(ref_ref.at[0], all_ref.at[me], ag_send_out.at[i - 1], ag_recv.at[me], out_peer(i)))
            for j in range(1, inner):
                pending.append(push(ref_ref.at[0], all_ref.at[me], ag_send_in.at[0, j - 1], ag_recv.at[me], in_peer(j)))
        core_copies.append(push(send_core.at[t], recv_core.at[t], core_send_sems.at[t], core_recv_sems.at[t], sibling))
        if t == 0:
            pending.append(push(ref_ref.at[0], all_ref.at[me], ag_send_core.at[0], ag_recv.at[me], sibling))
        else:
            inner_sends(t - 1)
        if t == CHUNKS - 1:
            wide = small_send.shape[2] // 2
            lane = lax.broadcasted_iota(jnp.int32, (rows, wide), 1).astype(jnp.float32)
            hits = jnp.where(lane == cls_col, 1.0, 0.0)
            small_send[0, :, :wide] = jnp.sum(hits, axis=0, keepdims=True)
            small_send[0, :, wide:] = jnp.sum(hits * wedge_sum, axis=0, keepdims=True)
        if t == 1:
            for i in range(1, outer):
                place = device(lax.rem(a + outer - i, outer), b, core)
                arrived(place)
                for j in range(1, inner):
                    pending.append(push(all_ref.at[place], all_ref.at[place], ag_send_in.at[i, j - 1], ag_recv.at[place], in_peer(j)))
                pending.append(push(all_ref.at[place], all_ref.at[place], ag_send_core.at[i], ag_recv.at[place], sibling))

    small = [push(small_send.at[0], small_recv.at[0], small_send_sems.at[0], small_recv_sems.at[0], sibling)]
    inner_sends(CHUNKS - 1)
    small[0].wait_recv()
    small_send[1] = small_send[0] + small_recv[0]

    own = [outer_sends(0)]
    for j in range(1, inner):
        small.append(push(small_send.at[1], small_recv.at[j], small_send_sems.at[j], small_recv_sems.at[j], in_peer(j)))

    slot = outer
    for i in range(outer):
        for j in range(1, inner):
            place = device(lax.rem(a + outer - i, outer), lax.rem(b + inner - j, inner), core)
            arrived(place)
            pending.append(push(all_ref.at[place], all_ref.at[place], ag_send_core.at[slot], ag_recv.at[place], sibling))
            slot += 1

    for t in range(1, CHUNKS - 1):
        own.append(outer_sends(t))
    tally = small_send[1]
    for j in range(1, inner):
        small[j].wait_recv()
        tally = tally + small_recv[j]
    small_send[2] = tally

    for i in range(outer):
        for j in range(inner):
            arrived(device(lax.rem(a + i, outer), lax.rem(b + j, inner), 1 - core))
    local.wait()
    nt = (((1,), (1,)), ((), ()))
    group = min(classes, 32)
    for g in range(classes // group):
        inter = jnp.zeros((rows, group), jnp.float32)
        energy = jnp.zeros((rows, group), jnp.float32)
        lines = slice(g * group, (g + 1) * group)
        for t in range(CHUNKS):
            cols = slice(t * span, (t + 1) * span)
            real = all_ref[lines, 0, cols].astype(jnp.float32)
            imag = all_ref[lines, 1, cols].astype(jnp.float32)
            ref_power = (real * real + imag * imag).astype(jnp.bfloat16)
            inter = inter + lax.dot_general(data[t, :, :span], real.astype(jnp.bfloat16), nt, preferred_element_type=jnp.float32)
            inter = inter + lax.dot_general(data[t, :, span:2 * span], imag.astype(jnp.bfloat16), nt, preferred_element_type=jnp.float32)
            energy = energy + lax.dot_general(low[:, cols], ref_power, nt, preferred_element_type=jnp.float32)
        scores_ref[:, lines] = inter / (
            math.sqrt(coef) * jnp.sqrt((energy / coef + EPS) * (power / coef + EPS)))

    own.append(outer_sends(CHUNKS - 1))
    for i in range(1, outer):
        at = inner + i - 1
        small.append(push(small_send.at[2], small_recv.at[at], small_send_sems.at[at], small_recv_sems.at[at], out_peer(i)))
    for i in range(1, outer):
        small[inner + i - 1].wait_recv()
        tally = tally + small_recv[inner + i - 1]
    wide = tally.shape[1] // 2
    load_ref[...] = tally[:, :classes] * classes / total
    lane = lax.broadcasted_iota(jnp.int32, (1, wide), 1)
    wedge_total = jnp.sum(jnp.where(lane == me, tally[:, wide:], 0.0), axis=1, keepdims=True)
    floor = TAU * (wedge_total / coef + 1.0)
    for t in range(CHUNKS):
        for copy in out_copies[t]:
            copy.wait_recv()
        whole = own[t]
        for i in range(1, outer):
            whole = whole + recv_out[t, i - 1].astype(jnp.float32)
        flat = jnp.concatenate([whole[0:1], whole[1:2]], axis=1)
        scale = 1.0 / (flat[:, 2 * span:] + floor)
        width = min(span, coef - t * span)
        for q in range(2):
            mean = flat[:, q * span:(q + 1) * span] * scale
            means_ref[0, q:q + 1, t * span:t * span + width] = mean[:, :width]

    for copy in pending + core_copies + small + sum(in_copies, []) + sum(out_copies, []):
        copy.wait_send()


def body(particles, references, assignment, orientation, tilt_range):
    part_rows = particles.shape[0]
    coef = particles.shape[2]
    devices = lax.axis_size("dom")
    classes = references.shape[0] * devices
    assert references.shape[0] == 1
    outer, inner = factor(devices)
    total = part_rows * devices
    unit = math.lcm(2 * LANES, SUB)
    span = -(-coef // (CHUNKS * unit)) * unit
    padded = CHUNKS * span
    width = 2 * (-(-classes // LANES) * LANES)
    parts = jnp.pad(jnp.transpose(particles, (1, 0, 2)), ((0, 0), (0, 0), (0, padded - coef)))
    refs = jnp.pad(references, ((0, 0), (0, 0), (0, padded - coef)))

    vmem = pl.BlockSpec(memory_space=pltpu.VMEM)
    dma = pltpu.SemaphoreType.DMA
    bf16, f32 = jnp.bfloat16, jnp.float32
    wide = 3 * span
    scores, means, load = pl.pallas_call(
        functools.partial(kernel, outer, inner, span, coef, total),
        out_shape=(
            jax.ShapeDtypeStruct((part_rows, classes), f32),
            jax.ShapeDtypeStruct((1, 2, coef), f32),
            jax.ShapeDtypeStruct((1, classes), f32),
        ),
        in_specs=[vmem] * 5,
        out_specs=(vmem, vmem, vmem),
        scratch_shapes=[
            pltpu.VMEM((CHUNKS, part_rows, wide), bf16),
            pltpu.VMEM((part_rows, padded), bf16),
            pltpu.VMEM((classes, 2, padded), bf16),
            pltpu.VMEM((CHUNKS, classes // 2, wide), f32),
            pltpu.VMEM((CHUNKS, classes // 2, wide), bf16),
            pltpu.VMEM((CHUNKS, classes // 2, wide), bf16),
            pltpu.VMEM((CHUNKS, inner - 1, outer, wide), bf16),
            pltpu.VMEM((CHUNKS, inner - 1, outer, wide), bf16),
            pltpu.VMEM((CHUNKS, outer - 1, 2, wide // 2), bf16),
            pltpu.VMEM((CHUNKS, outer - 1, 2, wide // 2), bf16),
            pltpu.VMEM((3, 1, width), f32),
            pltpu.VMEM((inner + outer - 1, 1, width), f32),
            dma((outer,)), dma((outer, inner)), dma((outer * inner,)), dma((classes,)),
            dma((CHUNKS,)), dma((CHUNKS,)),
            dma((CHUNKS, inner)), dma((CHUNKS, inner)), dma((CHUNKS, outer)), dma((CHUNKS, outer)),
            dma((inner + outer,)), dma((inner + outer,)), dma,
        ],
        compiler_params=pltpu.CompilerParams(
            collective_id=0, has_side_effects=True, vmem_limit_bytes=60 * 1024 * 1024
        ),
    )(parts, refs, assignment.reshape(1, part_rows), orientation[None, :], tilt_range)
    return (scores, means, load[0])


def solution(mesh):
    in_specs = (
        P("dom", None, None),
        P("dom", None, None),
        P("dom", None),
        P("dom"),
        P(None, "dom"),
    )
    out_specs = (P("dom", None), P("dom", None, None), P())
    return jax.shard_map(body, mesh=mesh, in_specs=in_specs, out_specs=out_specs, check_vma=False)
```

time: 40.7 us -> 39.6 us (0.973)
  other arithmetic: 9.56 us -> 0 us
  Pallas kernels: 26.7 us -> 32.4 us
  local copies, waits for them, and re-layouts: 1.4 us -> 6.27 us
  matrix products: 1.89 us -> 0 us
    pallas_call x1, Pallas kernels: 26.7 us -> 32.4 us  [body(): pl.pallas_call(functools.partial(kernel, outer, inner, span, coef, total)...]
    convert_element_type x6 -> x0, other arithmetic: 5.57 us -> none  [the longest x1 1.86 us: body(): p32 = piece.astype(jnp.float32)]
    unnamed x18 -> x8, local copies, waits for them, and re-layouts: 1.31 us -> 4.59 us
    dot_general x2 -> x0, matrix products: 1.89 us -> none  [the longest x1 1.5 us: body(): lax.dot_general(wedge_low, ref_power, (((1,), (1,)), ((), ())), preferred...]
    pad x0 -> x2, local copies, waits for them, and re-layouts: none -> 1.68 us  [the longest x1 1.04 us: body(): jnp.pad(jnp.transpose(particles, (1, 0, 2)), ((0, 0), (0, 0), (0, padded...]
    reduce_sum x2 -> x0, other arithmetic: 1.19 us -> none  [the longest x1 1.08 us: body(): power = jnp.sum(wedge * (pf[:, 0] * pf[:, 0] + pf[:, 1] * pf[:, 1]), axis=1)]
    cos x1 -> x0, other arithmetic: 0.81 us -> none  [wedge_weights(): jnp.cos(centre)]
    sin x1 -> x0, other arithmetic: 0.7 us -> none  [wedge_weights(): jnp.sin(angle)[:, None]]
where the time goes in v2:
time: 39.6 us; the launch traced here: 39.3 us
  Pallas kernels  32.4 us (82%)
  local copies, waits for them, and re-layouts  6.27 us (16%)
  between operations  0.65 us (2%)
    pallas_call x1, Pallas kernels, body(): pl.pallas_call(functools.partial(kernel, outer, inner, span, coef, total)...  32.4 us
    unnamed x8, local copies, waits for them, and re-layouts  4.59 us
    pad x1, local copies, waits for them, and re-layouts, body(): jnp.pad(jnp.transpose(particles, (1, 0, 2)), ((0, 0), (0, 0), (0, padded...  1.04 us

profile of v2, /device:TPU:0, one launch (start us, length us, event | category | flops | bytes accessed | tf_op | source)
XLA Modules:
  0.0 39.3 jit_solution(11304451910088584333)
XLA Ops:
  0.6 1.3 %copy.10 = bf16[32,2,7488]{2,0,1:T(8,128)(2,1)S(1)} copy(bf16[32,2,7488]{2,1,0:T(2,128)(2,1)} %param.5) | data formatting | bytes 1916928 | tf_op args[0]
  1.9 0.0 copy-start
  1.9 1.0 %pad.8.part_ref = bf16[2,32,7680]{2,1,0:T(8,128)(2,1)} pad(bf16[2,32,7488]{2,1,0:T(8,128)(2,1)S(1)} %bitcast.6, bf16[]{:T(256)} %constant.2.clone.1), padding=0_0x0_0x0_192 | pad | bytes 1941506 | tf_op jit(solution)/shard_map/jit(_pad)/pad | solution.py:293
  3.0 0.0 copy-done
  3.0 0.6 %pad.9.ref_ref = bf16[1,2,7680]{2,1,0:T(2,128)(2,1)} pad(bf16[1,2,7488]{2,1,0:T(2,128)(2,1)S(1)} %copy-done, bf16[]{:T(256)} %constant.2.clone.1), padding=0_0x0_0x0_192 | pad | bytes 60674 | tf_op jit(solution)/shard_map/jit(_pad)/pad | solution.py:294
  3.6 32.4 %shard_map.76 = (f32[32,32]{1,0:T(8,128)}, f32[1,2,7488]{2,1,0:T(2,128)}, f32[1,32]{1,0:T(1,128)}) custom-call(bf16[2,32,7680]{2,1,0:T(8,128)(2,1)} %pad.8.part_ref, bf16[1,2,7680]{2,1,0:T(2,128)(2,1)} %pad.9.ref_ref, s32[1,32]{1,0:T(1,128)} %bitcast.7, s32[1,32]{1,0:T(1,128)} %bitcast.8, s32[2,32]{1,0:T(2,128)} %tilt_ref.1), custom_call_target="tpu_custom_call" | custom-call | tf_op jit(solution)/shard_map/pallas_call | solution.py:300
  36.0 1.3 %copy.14 = f32[32,32]{1,0:T(8,128)} copy(f32[32,32]{1,0:T(8,128)} %get-tuple-element.12) | data formatting | bytes 8192
  37.3 0.0 copy-start.1
  37.3 1.5 %copy.15 = f32[1,2,7488]{2,1,0:T(2,128)} copy(f32[1,2,7488]{2,1,0:T(2,128)} %get-tuple-element.13) | data formatting | bytes 119808
  38.8 0.0 copy-done.1
  38.8 0.5 %copy.16 = f32[32]{0:T(128)} copy(f32[32]{0:T(128)S(1)} %bitcast.9) | data formatting | bytes 256
Async XLA Ops:
  1.9 1.1 %copy-start = (bf16[1,2,7488]{2,1,0:T(2,128)(2,1)S(1)}, bf16[1,2,7488]{2,1,0:T(2,128)(2,1)}, u32[]{:S(2)}) copy-start(bf16[1,2,7488]{2,1,0:T(2,128)(2,1)} %param.6) | copy-start | bytes 89860
  37.3 1.5 %copy-start.1 = (f32[1,32]{1,0:T(1,128)S(1)}, f32[1,32]{1,0:T(1,128)}, u32[]{:S(2)}) copy-start(f32[1,32]{1,0:T(1,128)} %get-tuple-element.8) | copy-start | bytes 388

commit v3 on v2

--- a/solution.py
+++ b/solution.py
@@ -65,7 +65,7 @@
     sibling = me + 1 - 2 * core
     classes = 2 * outer * inner
     half = classes // 2
-    rows = part_ref.shape[1]
+    rows = part_ref.shape[0]
 
     def device(a_at, b_at, c_at):
         return (a_at * inner + b_at) * 2 + c_at
@@ -153,6 +153,17 @@
                 out_send_sems.at[t, i - 1], out_recv_sems.at[t, i - 1], out_peer(i)))
         return jnp.concatenate([piece[0:1, :wide], piece[0:1, wide:]], axis=0)
 
+    def parts(first):
+        width = max(0, min(SUB, coef - first))
+        pieces = []
+        if width:
+            both = part_ref[:, :, first:first + width].astype(jnp.float32)
+            pieces.append(jnp.swapaxes(both, 0, 1))
+        if width < SUB:
+            pieces.append(jnp.zeros((2, rows, SUB - width), jnp.float32))
+        both = jnp.concatenate(pieces, axis=2) if len(pieces) > 1 else pieces[0]
+        return both[0], both[1]
+
     for t in range(CHUNKS):
         for s in range(span // SUB):
             first = t * span + s * SUB
@@ -163,8 +174,7 @@
             scale = 1.0 / (along_sq + (z_sq + 1.0))
             value = ((along_sq - z_sq) * cos_c - (2.0 * along * freq_z) * sin_c) * scale - cos_w
             wedge = 1.0 / (1.0 + jnp.exp(value * (-GAIN)))
-            real = part_ref[0, :, first:first + SUB].astype(jnp.float32)
-            imag = part_ref[1, :, first:first + SUB].astype(jnp.float32)
+            real, imag = parts(first)
             power = power + jnp.sum(wedge * (real * real + imag * imag), axis=1, keepdims=True)
             inside = wedge if first + SUB <= coef else jnp.where(index < coef, wedge, 0.0)
             wedge_sum = wedge_sum + jnp.sum(inside, axis=1, keepdims=True)
@@ -195,15 +205,14 @@
             hits = jnp.where(lane == cls_col, 1.0, 0.0)
             small_send[0, :, :wide] = jnp.sum(hits, axis=0, keepdims=True)
             small_send[0, :, wide:] = jnp.sum(hits * wedge_sum, axis=0, keepdims=True)
-        if t == 1:
-            for i in range(1, outer):
-                place = device(lax.rem(a + outer - i, outer), b, core)
-                arrived(place)
-                for j in range(1, inner):
-                    pending.append(push(all_ref.at[place], all_ref.at[place], ag_send_in.at[i, j - 1], ag_recv.at[place], in_peer(j)))
-                pending.append(push(all_ref.at[place], all_ref.at[place], ag_send_core.at[i], ag_recv.at[place], sibling))
-
     small = [push(small_send.at[0], small_recv.at[0], small_send_sems.at[0], small_recv_sems.at[0], sibling)]
+    for i in range(1, outer):
+        place = device(lax.rem(a + outer - i, outer), b, core)
+        arrived(place)
+        for j in range(1, inner):
+            pending.append(push(all_ref.at[place], all_ref.at[place], ag_send_in.at[i, j - 1], ag_recv.at[place], in_peer(j)))
+        pending.append(push(all_ref.at[place], all_ref.at[place], ag_send_core.at[i], ag_recv.at[place], sibling))
+
     inner_sends(CHUNKS - 1)
     small[0].wait_recv()
     small_send[1] = small_send[0] + small_recv[0]
@@ -232,6 +241,10 @@
         for j in range(inner):
             arrived(device(lax.rem(a + i, outer), lax.rem(b + j, inner), 1 - core))
     local.wait()
+    own.append(outer_sends(CHUNKS - 1))
+    for i in range(1, outer):
+        at = inner + i - 1
+        small.append(push(small_send.at[2], small_recv.at[at], small_send_sems.at[at], small_recv_sems.at[at], out_peer(i)))
     nt = (((1,), (1,)), ((), ()))
     group = min(classes, 32)
     for g in range(classes // group):
@@ -239,20 +252,16 @@
         energy = jnp.zeros((rows, group), jnp.float32)
         lines = slice(g * group, (g + 1) * group)
         for t in range(CHUNKS):
-            cols = slice(t * span, (t + 1) * span)
-            real = all_ref[lines, 0, cols].astype(jnp.float32)
-            imag = all_ref[lines, 1, cols].astype(jnp.float32)
+            width = min(span, coef - t * span)
+            cols = slice(t * span, t * span + width)
+            both = jnp.swapaxes(all_ref[lines, :, cols].astype(jnp.float32), 0, 1)
+            real, imag = both[0], both[1]
             ref_power = (real * real + imag * imag).astype(jnp.bfloat16)
-            inter = inter + lax.dot_general(data[t, :, :span], real.astype(jnp.bfloat16), nt, preferred_element_type=jnp.float32)
-            inter = inter + lax.dot_general(data[t, :, span:2 * span], imag.astype(jnp.bfloat16), nt, preferred_element_type=jnp.float32)
+            inter = inter + lax.dot_general(data[t, :, :width], real.astype(jnp.bfloat16), nt, preferred_element_type=jnp.float32)
+            inter = inter + lax.dot_general(data[t, :, span:span + width], imag.astype(jnp.bfloat16), nt, preferred_element_type=jnp.float32)
             energy = energy + lax.dot_general(low[:, cols], ref_power, nt, preferred_element_type=jnp.float32)
         scores_ref[:, lines] = inter / (
             math.sqrt(coef) * jnp.sqrt((energy / coef + EPS) * (power / coef + EPS)))
-
-    own.append(outer_sends(CHUNKS - 1))
-    for i in range(1, outer):
-        at = inner + i - 1
-        small.append(push(small_send.at[2], small_recv.at[at], small_send_sems.at[at], small_recv_sems.at[at], out_peer(i)))
     for i in range(1, outer):
         small[inner + i - 1].wait_recv()
         tally = tally + small_recv[inner + i - 1]
@@ -278,6 +287,21 @@
         copy.wait_send()
 
 
+def finish(*arrays):
+    def put(*refs):
+        for src, dst in zip(refs[:len(arrays)], refs[len(arrays):]):
+            dst[...] = src[...]
+
+    vmem = pl.BlockSpec(memory_space=pltpu.VMEM)
+    scores, means, load = pl.pallas_call(
+        put,
+        out_shape=tuple(jax.ShapeDtypeStruct(x.shape, x.dtype) for x in arrays),
+        in_specs=[vmem] * len(arrays),
+        out_specs=(vmem,) * len(arrays),
+    )(*arrays)
+    return (scores, means, load[0])
+
+
 def body(particles, references, assignment, orientation, tilt_range):
     part_rows = particles.shape[0]
     coef = particles.shape[2]
@@ -290,8 +314,6 @@
     span = -(-coef // (CHUNKS * unit)) * unit
     padded = CHUNKS * span
     width = 2 * (-(-classes // LANES) * LANES)
-    parts = jnp.pad(jnp.transpose(particles, (1, 0, 2)), ((0, 0), (0, 0), (0, padded - coef)))
-    refs = jnp.pad(references, ((0, 0), (0, 0), (0, padded - coef)))
 
     vmem = pl.BlockSpec(memory_space=pltpu.VMEM)
     dma = pltpu.SemaphoreType.DMA
@@ -309,7 +331,7 @@
         scratch_shapes=[
             pltpu.VMEM((CHUNKS, part_rows, wide), bf16),
             pltpu.VMEM((part_rows, padded), bf16),
-            pltpu.VMEM((classes, 2, padded), bf16),
+            pltpu.VMEM((classes, 2, coef), bf16),
             pltpu.VMEM((CHUNKS, classes // 2, wide), f32),
             pltpu.VMEM((CHUNKS, classes // 2, wide), bf16),
             pltpu.VMEM((CHUNKS, classes // 2, wide), bf16),
@@ -327,8 +349,8 @@
         compiler_params=pltpu.CompilerParams(
             collective_id=0, has_side_effects=True, vmem_limit_bytes=60 * 1024 * 1024
         ),
-    )(parts, refs, assignment.reshape(1, part_rows), orientation[None, :], tilt_range)
-    return (scores, means, load[0])
+    )(particles, references, assignment.reshape(1, part_rows), orientation[None, :], tilt_range)
+    return finish(scores, means, load)
 
 
 def solution(mesh):

time: 39.6 us -> 30.8 us (0.78)
  local copies, waits for them, and re-layouts: 6.27 us -> 0 us
  Pallas kernels: 32.4 us -> 30 us
    unnamed x8 -> x0, local copies, waits for them, and re-layouts: 4.59 us -> none
    pallas_call x1, Pallas kernels: 32.4 us -> 28.6 us  [body(): pl.pallas_call(functools.partial(kernel, outer, inner, span, coef, total)...]
    pad x2 -> x0, local copies, waits for them, and re-layouts: 1.68 us -> none  [the longest x1 1.04 us: body(): jnp.pad(jnp.transpose(particles, (1, 0, 2)), ((0, 0), (0, 0), (0, padded...]
    pallas_call x0 -> x1, Pallas kernels: none -> 1.46 us  [finish(): pl.pallas_call(put, out_shape=tuple((jax.ShapeDtypeStruct(x.shape, x.dtyp...]
where the time goes in v3:
time: 30.8 us; the launch traced here: 30.7 us
  Pallas kernels  30 us (97%)
  between operations  0.64 us (2%)
    pallas_call x1, Pallas kernels, body(): pl.pallas_call(functools.partial(kernel, outer, inner, span, coef, total)...  28.6 us
    pallas_call x1, Pallas kernels, finish(): pl.pallas_call(put, out_shape=tuple((jax.ShapeDtypeStruct(x.shape, x.dtyp...  1.46 us

profile of v3, /device:TPU:0, one launch (start us, length us, event | category | flops | bytes accessed | tf_op | source)
XLA Modules:
  0.0 30.7 jit_solution(17342241605497985002)
XLA Ops:
  0.6 28.6 %shard_map.76 = (f32[32,32]{1,0:T(8,128)}, f32[1,2,7488]{2,1,0:T(2,128)}, f32[1,32]{1,0:T(1,128)}) custom-call(bf16[32,2,7488]{2,1,0:T(2,128)(2,1)} %part_ref.1, bf16[1,2,7488]{2,1,0:T(2,128)(2,1)} %ref_ref.1, s32[1,32]{1,0:T(1,128)} %bitcast.3, s32[1,32]{1,0:T(1,128)} %bitcast.4, s32[2,32]{1,0:T(2,128)} %tilt_ref.1), custom_call_target="tpu_custom_call" | custom-call | tf_op jit(solution)/shard_map/pallas_call | solution.py:322
  29.2 1.5 %shard_map.77 = (f32[32,32]{1,0:T(8,128)}, f32[1,2,7488]{2,1,0:T(2,128)}, f32[1,32]{1,0:T(1,128)}) custom-call(f32[32,32]{1,0:T(8,128)} %get-tuple-element.9.refs_0_, f32[1,2,7488]{2,1,0:T(2,128)} %get-tuple-element.10.refs_1_, f32[1,32]{1,0:T(1,128)} %get-tuple-element.11.refs_2_), custom_call_target="tpu_custom_call" | custom-call | tf_op jit(solution)/shard_map/pallas_call | solution.py:296

commit v4 on v3

--- a/solution.py
+++ b/solution.py
@@ -206,6 +206,13 @@
             small_send[0, :, :wide] = jnp.sum(hits, axis=0, keepdims=True)
             small_send[0, :, wide:] = jnp.sum(hits * wedge_sum, axis=0, keepdims=True)
     small = [push(small_send.at[0], small_recv.at[0], small_send_sems.at[0], small_recv_sems.at[0], sibling)]
+    inner_sends(CHUNKS - 1)
+    small[0].wait_recv()
+    small_send[1] = small_send[0] + small_recv[0]
+
+    for j in range(1, inner):
+        small.append(push(small_send.at[1], small_recv.at[j], small_send_sems.at[j], small_recv_sems.at[j], in_peer(j)))
+
     for i in range(1, outer):
         place = device(lax.rem(a + outer - i, outer), b, core)
         arrived(place)
@@ -213,14 +220,16 @@
             pending.append(push(all_ref.at[place], all_ref.at[place], ag_send_in.at[i, j - 1], ag_recv.at[place], in_peer(j)))
         pending.append(push(all_ref.at[place], all_ref.at[place], ag_send_core.at[i], ag_recv.at[place], sibling))
 
-    inner_sends(CHUNKS - 1)
-    small[0].wait_recv()
-    small_send[1] = small_send[0] + small_recv[0]
-
-    own = [outer_sends(0)]
+    own = [outer_sends(t) for t in range(CHUNKS)]
+    tally = small_send[1]
     for j in range(1, inner):
-        small.append(push(small_send.at[1], small_recv.at[j], small_send_sems.at[j], small_recv_sems.at[j], in_peer(j)))
-
+        small[j].wait_recv()
+        tally = tally + small_recv[j]
+    small_send[2] = tally
+
+    for i in range(1, outer):
+        at = inner + i - 1
+        small.append(push(small_send.at[2], small_recv.at[at], small_send_sems.at[at], small_recv_sems.at[at], out_peer(i)))
     slot = outer
     for i in range(outer):
         for j in range(1, inner):
@@ -229,22 +238,10 @@
             pending.append(push(all_ref.at[place], all_ref.at[place], ag_send_core.at[slot], ag_recv.at[place], sibling))
             slot += 1
 
-    for t in range(1, CHUNKS - 1):
-        own.append(outer_sends(t))
-    tally = small_send[1]
-    for j in range(1, inner):
-        small[j].wait_recv()
-        tally = tally + small_recv[j]
-    small_send[2] = tally
-
     for i in range(outer):
         for j in range(inner):
             arrived(device(lax.rem(a + i, outer), lax.rem(b + j, inner), 1 - core))
     local.wait()
-    own.append(outer_sends(CHUNKS - 1))
-    for i in range(1, outer):
-        at = inner + i - 1
-        small.append(push(small_send.at[2], small_recv.at[at], small_send_sems.at[at], small_recv_sems.at[at], out_peer(i)))
     nt = (((1,), (1,)), ((), ()))
     group = min(classes, 32)
     for g in range(classes // group):

time: 30.8 us -> 28.7 us (0.932)
  Pallas kernels: 30 us -> 27.9 us
    pallas_call x1, Pallas kernels: 28.6 us -> 26.4 us  [body(): pl.pallas_call(functools.partial(kernel, outer, inner, span, coef, total)...]
where the time goes in v4:
time: 28.7 us; the launch traced here: 28.5 us
  Pallas kernels  27.9 us (97%)
  between operations  0.64 us (2%)
    pallas_call x1, Pallas kernels, body(): pl.pallas_call(functools.partial(kernel, outer, inner, span, coef, total)...  26.4 us
    pallas_call x1, Pallas kernels, finish(): pl.pallas_call(put, out_shape=tuple((jax.ShapeDtypeStruct(x.shape, x.dtyp...  1.46 us

profile of v4, /device:TPU:0, one launch (start us, length us, event | category | flops | bytes accessed | tf_op | source)
XLA Modules:
  0.0 28.5 jit_solution(9527285882644175699)
XLA Ops:
  0.6 26.4 %shard_map.76 = (f32[32,32]{1,0:T(8,128)}, f32[1,2,7488]{2,1,0:T(2,128)}, f32[1,32]{1,0:T(1,128)}) custom-call(bf16[32,2,7488]{2,1,0:T(2,128)(2,1)} %part_ref.1, bf16[1,2,7488]{2,1,0:T(2,128)(2,1)} %ref_ref.1, s32[1,32]{1,0:T(1,128)} %bitcast.3, s32[1,32]{1,0:T(1,128)} %bitcast.4, s32[2,32]{1,0:T(2,128)} %tilt_ref.1), custom_call_target="tpu_custom_call" | custom-call | tf_op jit(solution)/shard_map/pallas_call | solution.py:319
  27.0 1.5 %shard_map.77 = (f32[32,32]{1,0:T(8,128)}, f32[1,2,7488]{2,1,0:T(2,128)}, f32[1,32]{1,0:T(1,128)}) custom-call(f32[32,32]{1,0:T(8,128)} %get-tuple-element.9.refs_0_, f32[1,2,7488]{2,1,0:T(2,128)} %get-tuple-element.10.refs_1_, f32[1,32]{1,0:T(1,128)} %get-tuple-element.11.refs_2_), custom_call_target="tpu_custom_call" | custom-call | tf_op jit(solution)/shard_map/pallas_call | solution.py:293
